TPU v7x, 16 devices: a whole 2x2x2 slice. The times are simulated.
16 devices in a mesh: dp: 1, tp: 16 (over x, y, z, core).
Axes of the slice: x: 2, y: 2, z: 2, core: 2. Of those that a mesh axis runs over, the one named last changes fastest.
Arguments:
- x: bfloat16 [2048, 4096], P('dp')
- w_gate: bfloat16 [4096, 10240], P(None, 'tp')
- w_up: bfloat16 [4096, 10240], P(None, 'tp')
- w_down: bfloat16 [10240, 4096], P('tp')
Outputs:
- output: bfloat16 [2048, 4096], P('dp')
All inputs are finite; a program needn't handle non-finite values.
Results may differ from a plain program's by a relative error of at most 0.016.
Values are sent between devices in bfloat16 or wider.
A program may use at most 2 GiB of HBM per device.

v0:
```python
import jax
import jax.numpy as jnp
from jax import lax
from jax.sharding import PartitionSpec as P


def solution(mesh):
    def step(x, w_gate, w_up, w_down):
        gate = jnp.dot(x, w_gate, preferred_element_type=jnp.float32)
        up = jnp.dot(x, w_up, preferred_element_type=jnp.float32)
        hidden = (jax.nn.gelu(gate) * up).astype(jnp.bfloat16)
        term = jnp.dot(hidden, w_down, preferred_element_type=jnp.float32).astype(jnp.bfloat16)
        return lax.psum(term, "tp")

    return jax.shard_map(
        step,
        mesh=mesh,
        in_specs=(P("dp", None), P(None, "tp"), P(None, "tp"), P("tp", None)),
        out_specs=P("dp", None),
        check_vma=False,
    )
```

profile of v0, /device:TPU:0, one launch (start us, length us, event | category | flops | bytes accessed | tf_op | source)
XLA Modules:
  0.0 263.8 jit_solution(529681825926917647)
XLA Ops:
  6.5 0.0 all-reduce.2.cloned.1.call-start
  6.5 0.0 copy-start
  6.5 0.0 copy-start.1
  6.5 0.0 slice-start
  6.5 19.1 %fusion.9 = f32[2048,640]{1,0:T(8,128)} fusion(bf16[2048,4096]{1,0:T(8,128)(2,1)} %param.4, bf16[4096,640]{1,0:T(8,128)(2,1)} %param.5), kind=kOutput, calls=%fused_computation.11 | convolution fusion | flops 10737418240 | bytes 27262976 | tf_op jit(solution)/shard_map/dot_general | solution.py:9
  25.6 0.0 copy-done
  25.6 0.0 copy-done.1
  25.6 0.0 slice-start.1
  25.6 16.8 %fusion.8 = bf16[2048,640]{1,0:T(8,128)(2,1)} fusion(f32[2048,640]{1,0:T(8,128)} %fusion.9, bf16[2048,4096]{1,0:T(8,128)(2,1)S(1)} %copy-done, bf16[4096,640]{1,0:T(8,128)(2,1)S(1)} %copy-done.1), kind=kOutput, calls=%fused_computation.10 | convolution fusion | flops 10750525440 | bytes 29884416 | tf_op jit(solution)/shard_map/dot_general | solution.py:10
  42.5 0.0 slice-done
  42.5 0.0 slice-done.1
  42.5 17.6 %convolution_convert_fusion = bf16[2048,4096]{1,0:T(8,128)(2,1)} fusion(bf16[2048,640]{1,0:T(8,128)(2,1)} %fusion.8, bf16[640,4096]{1,0:T(8,128)(2,1)S(1)} %bitcast.7), kind=kOutput, calls=%fused_computation | convolution fusion | flops 10745806848 | bytes 24641536 | tf_op jit(solution)/shard_map/dot_general | solution.py:12
  60.0 0.0 all-reduce.2.cloned.1.call-update
  60.1 182.8 %all-reduce.2.cloned.1.call-done = bf16[2048,4096]{1,0:T(8,128)(2,1)} async-done(((bf16[2048,4096]{1,0:T(8,128)(2,1)}), bf16[2048,4096]{1,0:T(8,128)(2,1)}) %all-reduce.2.cloned.1.call-update) | async-done | bytes 16777232 | tf_op jit(solution)/shard_map/psum | solution.py:13
  242.9 14.1 %copy.6 = bf16[2048,4096]{1,0:T(8,128)(2,1)} copy(bf16[2048,4096]{1,0:T(8,128)(2,1)} %all-reduce.2.cloned.1.call-done) | data formatting | bytes 33554432
  (1 shorter events, 0.0 us)
Async XLA Ops:
  6.5 236.4 %all-reduce.2.cloned.1.call-start = ((), (), s32[]{:S(2)}) async-start(), calls=%async_computation | async-start | bytes 33554432 | tf_op jit(solution)/shard_map/psum | solution.py:13
  6.5 19.1 %copy-start = (bf16[2048,4096]{1,0:T(8,128)(2,1)S(1)}, bf16[2048,4096]{1,0:T(8,128)(2,1)}, u32[]{:S(2)}) copy-start(bf16[2048,4096]{1,0:T(8,128)(2,1)} %param.4) | copy-start | bytes 50331652
  6.5 19.1 %copy-start.1 = (bf16[4096,640]{1,0:T(8,128)(2,1)S(1)}, bf16[4096,640]{1,0:T(8,128)(2,1)}, u32[]{:S(2)}) copy-start(bf16[4096,640]{1,0:T(8,128)(2,1)} %param.6) | copy-start | bytes 15728644
  6.5 35.9 %slice-start = ((s8[5242880]{0:T(1024)(128)(4,1)}), s8[4194304]{0:T(1024)(128)(4,1)S(1)}, s32[]{:S(2)}) async-start(s8[5242880]{0:T(1024)(128)(4,1)} %bitcast.6), calls=%async_computation.1 | async-start | bytes 8388608
  25.6 16.9 %slice-start.1 = ((s8[5242880]{0:T(1024)(128)(4,1)}), s8[1048576]{0:T(1024)(128)(4,1)S(1)}, s32[]{:S(2)}) async-start(s8[5242880]{0:T(1024)(128)(4,1)} %bitcast.6), calls=%async_computation.2 | async-start | bytes 2097152
Sparse Core Ops, SparseCore 0:
  60.2 182.6 all-reduce.1
where the time goes:
time: 264 us
  waiting for transfers between devices  183 us (69%)
  matrix products  53.5 us (20%)
  local copies, waits for them, and re-layouts  14.1 us (5%)
  between operations  13.4 us (5%)
    psum x1, waiting for transfers between devices, step(): return lax.psum(term, 'tp')  183 us
    dot_general x1, matrix products, step(): gate = jnp.dot(x, w_gate, preferred_element_type=jnp.float32)  19.1 us
    dot_general x1, matrix products, step(): jnp.dot(hidden, w_down, preferred_element_type=jnp.float32)  17.6 us
    dot_general x1, matrix products, step(): up = jnp.dot(x, w_up, preferred_element_type=jnp.float32)  16.8 us
    unnamed x9, local copies, waits for them, and re-layouts  14.1 us
  transfers between devices with their start and end apart: 1, of which 1 were waited for; matrix products, arithmetic and copies ran while one was open for 0% of the time, Pallas kernels for 0%

commit v1 on v0

v1 whole, which is shorter than its diff:
```python
import functools

import jax
import jax.numpy as jnp
from jax import lax
from jax.experimental import pallas as pl
from jax.experimental.pallas import tpu as pltpu
from jax.sharding import PartitionSpec as P

MESH = pl.DeviceIdType.MESH
CHUNKS = 8
RING = 4


def kernel(
    cfg, x_ref, wg_ref, wu_ref, wd_ref, y_ref,
    xb, wgu, wd, h, hs, keep, s1, s2, s3, r1, r2, r3,
    xsem, wsem, wdl, wds, wdr, hss, hsr, ss, rs, fs, fr,
):
    n, R, ff, parts = cfg
    half, quarter, eighth = R // 2, R // 4, R // 8
    me = lax.axis_index("tp")
    core = lax.rem(me, 2)
    bits = (lax.div(me, 8), lax.rem(lax.div(me, 4), 2), lax.rem(lax.div(me, 2), 2))
    strides = (8, 4, 2)
    partner = me + 1 - 2 * core
    across = [me + s * (1 - 2 * b) for s, b in zip(strides, bits)]
    rows = n * R
    mine = core * rows
    other = (1 - core) * rows

    def dev(d):
        return {"tp": d}

    def bit(p, k):
        return bits[(p + k) % 3]

    def to(p, k):
        return dev(across[(p + k) % 3])

    def x_copies(i):
        slot = lax.rem(i, 2)
        return [
            pltpu.make_async_copy(
                x_ref.at[pl.ds(pl.multiple_of(start + i * R, R), R), :],
                xb.at[slot, pl.ds(j * R, R), :],
                xsem.at[slot, j],
            )
            for j, start in enumerate((mine, other))
        ]

    wg_copy = pltpu.make_async_copy(wg_ref, wgu.at[:, pl.ds(0, ff)], wsem.at[0])
    wu_copy = pltpu.make_async_copy(wu_ref, wgu.at[:, pl.ds(ff, ff)], wsem.at[1])
    wd_local = pltpu.make_async_copy(wd_ref, wd.at[pl.ds(0, ff), :], wdl.at[0])

    def wd_swap(p):
        c0, w = parts[p]
        return pltpu.make_async_remote_copy(
            wd_ref.at[:, pl.ds(c0, w)],
            wd.at[pl.ds(ff, ff), pl.ds(c0, w)],
            wds.at[p], wdr.at[p], device_id=dev(partner), device_id_type=MESH,
        )

    def h_swap(i):
        return pltpu.make_async_remote_copy(
            hs.at[lax.rem(i, 2)],
            h.at[i, :, pl.ds(ff, ff)],
            hss.at[i], hsr.at[i], device_id=dev(partner), device_id_type=MESH,
        )

    def y_rows(i, p, depth):
        start = mine + i * R
        size = R
        for k in range(depth):
            size //= 2
            start = start + bit(p, k) * size
        return pl.ds(pl.multiple_of(start, size), size)

    def hop(stage, i, p):
        c0, w = parts[p]
        cols = pl.ds(c0, w)
        slot = lax.rem(i, RING)
        if stage == 0:
            src, dst, k = s1.at[slot, :, cols], r1.at[i, :, cols], 0
        elif stage == 1:
            src, dst, k = s2.at[slot, :, cols], r2.at[i, :, cols], 1
        elif stage == 2:
            src, dst, k = s3.at[slot, :, cols], r3.at[i, :, cols], 2
        else:
            k = 5 - stage
            src = dst = y_ref.at[y_rows(i, p, k + 1), cols]
        return pltpu.make_async_remote_copy(
            src, dst, ss.at[stage, i, p], rs.at[stage, i, p],
            device_id=to(p, k), device_id_type=MESH,
        )

    def forward(i, p, late):
        c0, w = parts[p]
        b = bit(p, 0)
        start = mine + i * R + (1 - b if late else b) * half
        blk = y_ref.at[pl.ds(pl.multiple_of(start, half), half), pl.ds(c0, w)]
        return pltpu.make_async_remote_copy(
            blk, blk, fs.at[late, i, p], fr.at[late, i, p],
            device_id=dev(partner), device_id_type=MESH,
        )

    def gate_up(i):
        slot = lax.rem(i, 2)
        for c in x_copies(i):
            c.wait()
        gu = jnp.dot(xb[slot], wgu[...], preferred_element_type=jnp.float32)
        hid = (jax.nn.gelu(gu[:, :ff]) * gu[:, ff:]).astype(jnp.bfloat16)

        @pl.when(i >= 2)
        def _():
            h_swap(i - 2).wait_send()

        hs[slot] = hid[R:]
        h_swap(i).start()
        h[i, :, pl.ds(0, ff)] = hid[:R]

    def down(i):
        slot = lax.rem(i, RING)
        h_swap(i).wait_recv()
        for p in range(3):
            c0, w = parts[p]

            @pl.when(i == 0)
            def _():
                wd_swap(p).wait_recv()

            term = jnp.dot(
                h[i], wd[:, c0 : c0 + w], preferred_element_type=jnp.float32
            )
            b = bit(p, 0)
            top, bot = term[:half], term[half:]

            @pl.when(i >= RING)
            def _():
                hop(0, i - RING, p).wait_send()

            s1[slot, :, c0 : c0 + w] = jnp.where(b == 1, top, bot).astype(jnp.bfloat16)
            hop(0, i, p).start()
            keep[slot, :, c0 : c0 + w] = jnp.where(b == 1, bot, top)

    def reduce(stage, i):
        slot = lax.rem(i, RING)
        for p in range(3):
            c0, w = parts[p]
            cols = pl.ds(c0, w)
            hop(stage, i, p).wait_recv()
            b1, b2 = bit(p, 1), bit(p, 2)
            if stage == 0:
                o = pl.multiple_of((1 - b1) * quarter, quarter)
                v = keep[slot, pl.ds(o, quarter), cols]
                v = v + r1[i, pl.ds(o, quarter), cols].astype(jnp.float32)

                @pl.when(i >= RING)
                def _():
                    hop(1, i - RING, p).wait_send()

                s2[slot, :, cols] = v.astype(jnp.bfloat16)
                hop(1, i, p).start()
            else:
                b = 1 - b2 if stage == 1 else b2
                o1 = pl.multiple_of(b1 * quarter + b * eighth, eighth)
                o2 = pl.multiple_of(b * eighth, eighth)
                v = keep[slot, pl.ds(o1, eighth), cols]
                v = v + r1[i, pl.ds(o1, eighth), cols].astype(jnp.float32)
                v = v + r2[i, pl.ds(o2, eighth), cols].astype(jnp.float32)
                if stage == 1:

                    @pl.when(i >= RING)
                    def _():
                        hop(2, i - RING, p).wait_send()

                    s3[slot, :, cols] = v.astype(jnp.bfloat16)
                    hop(2, i, p).start()
                else:
                    v = v + r3[i, :, cols].astype(jnp.float32)
                    y_ref[y_rows(i, p, 3), cols] = v.astype(jnp.bfloat16)
                    hop(3, i, p).start()

    def gather(stage, i):
        for p in range(3):
            hop(stage, i, p).wait_recv()
            if stage < 5:
                hop(stage + 1, i, p).start()
            if stage >= 4:
                forward(i, p, stage - 4).start()

    for c in x_copies(0):
        c.start()
    wg_copy.start()
    wu_copy.start()
    wd_local.start()
    barrier = pltpu.get_barrier_semaphore()
    for d in [partner] + across:
        pl.semaphore_signal(barrier, inc=1, device_id=dev(d), device_id_type=MESH)
    pl.semaphore_wait(barrier, 4)
    for p in range(3):
        wd_swap(p).start()
    for c in x_copies(1):
        c.start()
    wg_copy.wait()
    wu_copy.wait()
    gate_up(0)
    wd_local.wait()

    def body(t, _):
        for stage in (5, 4, 3):
            i = t - 1 - stage

            @pl.when(jnp.logical_and(i >= 0, i < n))
            def _():
                gather(stage, i)

        for stage in (2, 1, 0):
            i = t - 1 - stage

            @pl.when(jnp.logical_and(i >= 0, i < n))
            def _():
                reduce(stage, i)

        @pl.when(t < n)
        def _():
            down(t)

        @pl.when(t + 1 < n)
        def _():
            @pl.when(t + 2 < n)
            def _():
                for c in x_copies(t + 2):
                    c.start()

            gate_up(t + 1)

        return 0

    lax.fori_loop(0, n + 6, body, 0)

    for p in range(3):
        wd_swap(p).wait_send()
    for i in range(n - 2, n):
        h_swap(i).wait_send()

    def drain(i, _):
        for p in range(3):
            for stage in range(3, 6):
                hop(stage, i, p).wait_send()
            for late in range(2):
                forward(i, p, late).wait_send()
                forward(i, p, late).wait_recv()
        return 0

    lax.fori_loop(0, n, drain, 0)
    for i in range(n - RING, n):
        for p in range(3):
            for stage in range(3):
                hop(stage, i, p).wait_send()


def solution(mesh):
    def step(x, w_gate, w_up, w_down):
        rows, d = x.shape
        ff = w_gate.shape[1]
        n = CHUNKS
        R = rows // 2 // n
        tiles = d // 128
        widths = [128 * (tiles // 3 + (1 if p < tiles % 3 else 0)) for p in range(3)]
        parts = tuple((sum(widths[:p]), widths[p]) for p in range(3))
        bf16, f32 = jnp.bfloat16, jnp.float32
        dma = pltpu.SemaphoreType.DMA
        return pl.pallas_call(
            functools.partial(kernel, (n, R, ff, parts)),
            name="mlp",
            out_shape=pltpu.VMEM((rows, d), bf16),
            in_specs=[pl.BlockSpec(memory_space=pltpu.HBM)] * 4,
            out_specs=pl.BlockSpec(memory_space=pltpu.VMEM),
            scratch_shapes=[
                pltpu.VMEM((2, 2 * R, d), bf16),
                pltpu.VMEM((d, 2 * ff), bf16),
                pltpu.VMEM((2 * ff, d), bf16),
                pltpu.VMEM((n, R, 2 * ff), bf16),
                pltpu.VMEM((2, R, ff), bf16),
                pltpu.VMEM((RING, R // 2, d), f32),
                pltpu.VMEM((RING, R // 2, d), bf16),
                pltpu.VMEM((RING, R // 4, d), bf16),
                pltpu.VMEM((RING, R // 8, d), bf16),
                pltpu.VMEM((n, R // 2, d), bf16),
                pltpu.VMEM((n, R // 4, d), bf16),
                pltpu.VMEM((n, R // 8, d), bf16),
                dma((2, 2)),
                dma((2,)),
                dma((1,)),
                dma((3,)),
                dma((3,)),
                dma((n,)),
                dma((n,)),
                dma((6, n, 3)),
                dma((6, n, 3)),
                dma((2, n, 3)),
                dma((2, n, 3)),
            ],
            compiler_params=pltpu.CompilerParams(
                collective_id=0,
                has_side_effects=True,
                vmem_limit_bytes=46 * 2**20,
            ),
            cost_estimate=pl.CostEstimate(
                flops=6 * rows * d * ff, bytes_accessed=50 * 2**20, transcendentals=0
            ),
        )(x, w_gate, w_up, w_down)

    return jax.shard_map(
        step,
        mesh=mesh,
        in_specs=(P("dp", None), P(None, "tp"), P(None, "tp"), P("tp", None)),
        out_specs=P("dp", None),
        check_vma=False,
    )
```

time: 264 us -> 139 us (0.53)
  waiting for transfers between devices: 183 us -> 0 us
  Pallas kernels: 0 us -> 133 us
  matrix products: 53.5 us -> 0 us
  between operations: 13.4 us -> 0.01 us
  local copies, waits for them, and re-layouts: 14.1 us -> 6.16 us
    psum x1 -> x0, waiting for transfers between devices: 183 us -> none  [step(): return lax.psum(term, 'tp')]
    pallas_call x0 -> x1, Pallas kernels: none -> 133 us  [step(): pl.pallas_call(functools.partial(kernel, (n, R, ff, parts)), name='mlp',...]
    dot_general x3 -> x0, matrix products: 53.5 us -> none  [the longest x1 19.1 us: step(): gate = jnp.dot(x, w_gate, preferred_element_type=jnp.float32)]
    unnamed x9 -> x1, local copies, waits for them, and re-layouts: 14.1 us -> 6.16 us
  transfers between devices with their start and end apart: 1 -> 0, of which waited for: 1 -> 0; matrix products, arithmetic and copies ran while one was open for 0% -> 0% of each run, Pallas kernels for 0% -> 0%
where the time goes in v1:
time: 139 us
  Pallas kernels  133 us (96%)
  local copies, waits for them, and re-layouts  6.16 us (4%)
    pallas_call x1, Pallas kernels, step(): pl.pallas_call(functools.partial(kernel, (n, R, ff, parts)), name='mlp',...  133 us
    unnamed x1, local copies, waits for them, and re-layouts  6.16 us

profile of v1, /device:TPU:0, one launch (start us, length us, event | category | flops | bytes accessed | tf_op | source)
XLA Modules:
  0.0 139.1 jit_solution(6372357679811738737)
XLA Ops:
  0.0 132.9 %mlp.1 = bf16[2048,4096]{1,0:T(8,128)(2,1)S(1)} custom-call(bf16[2048,4096]{1,0:T(8,128)(2,1)} %x_ref.1, bf16[4096,640]{1,0:T(8,128)(2,1)} %wg_ref.1, bf16[4096,640]{1,0:T(8,128)(2,1)} %wu_ref.1, bf16[640,4096]{1,0:T(8,128)(2,1)} %wd_ref.1), custom_call_target="tpu_custom_call" | custom-call | flops 32212254720 | bytes 52428800 | tf_op jit(solution)/shard_map/mlp/pallas_call | solution.py:274
  132.9 6.2 %copy.6 = bf16[2048,4096]{1,0:T(8,128)(2,1)} copy(bf16[2048,4096]{1,0:T(8,128)(2,1)S(1)} %mlp.1) | data formatting | bytes 33554432

commit v2 on v1

--- a/solution.py
+++ b/solution.py
@@ -9,22 +9,20 @@
 
 MESH = pl.DeviceIdType.MESH
 CHUNKS = 8
-RING = 4
+AHEAD = 2
+RINGS = (4, 4, 8)
 
 
 def kernel(
     cfg, x_ref, wg_ref, wu_ref, wd_ref, y_ref,
-    xb, wgu, wd, h, hs, keep, s1, s2, s3, r1, r2, r3,
+    xb, wgu, wd, h, hs, keep, s1, s2, s3, r2, r3,
     xsem, wsem, wdl, wds, wdr, hss, hsr, ss, rs, fs, fr,
 ):
     n, R, ff, parts = cfg
     half, quarter, eighth = R // 2, R // 4, R // 8
     me = lax.axis_index("tp")
     core = lax.rem(me, 2)
-    bits = (lax.div(me, 8), lax.rem(lax.div(me, 4), 2), lax.rem(lax.div(me, 2), 2))
-    strides = (8, 4, 2)
     partner = me + 1 - 2 * core
-    across = [me + s * (1 - 2 * b) for s, b in zip(strides, bits)]
     rows = n * R
     mine = core * rows
     other = (1 - core) * rows
@@ -32,11 +30,16 @@
     def dev(d):
         return {"tp": d}
 
-    def bit(p, k):
-        return bits[(p + k) % 3]
-
-    def to(p, k):
-        return dev(across[(p + k) % 3])
+    def stride(i, p, k):
+        a = lax.rem(i + p + k, 3)
+        return 8 - 4 * a + a * (a - 1)
+
+    def bit(i, p, k):
+        return lax.rem(lax.div(me, stride(i, p, k)), 2)
+
+    def to(i, p, k):
+        s = stride(i, p, k)
+        return dev(me + s * (1 - 2 * bit(i, p, k)))
 
     def x_copies(i):
         slot = lax.rem(i, 2)
@@ -73,15 +76,19 @@
         size = R
         for k in range(depth):
             size //= 2
-            start = start + bit(p, k) * size
+            start = start + bit(i, p, k) * size
         return pl.ds(pl.multiple_of(start, size), size)
 
     def hop(stage, i, p):
         c0, w = parts[p]
         cols = pl.ds(c0, w)
-        slot = lax.rem(i, RING)
+        if stage < 3:
+            slot = lax.rem(i, RINGS[stage])
         if stage == 0:
-            src, dst, k = s1.at[slot, :, cols], r1.at[i, :, cols], 0
+            k = 0
+            src = s1.at[slot, :, cols]
+            start = mine + i * R + (1 - bit(i, p, 0)) * half
+            dst = y_ref.at[pl.ds(pl.multiple_of(start, half), half), cols]
         elif stage == 1:
             src, dst, k = s2.at[slot, :, cols], r2.at[i, :, cols], 1
         elif stage == 2:
@@ -91,12 +98,12 @@
             src = dst = y_ref.at[y_rows(i, p, k + 1), cols]
         return pltpu.make_async_remote_copy(
             src, dst, ss.at[stage, i, p], rs.at[stage, i, p],
-            device_id=to(p, k), device_id_type=MESH,
+            device_id=to(i, p, k), device_id_type=MESH,
         )
 
     def forward(i, p, late):
         c0, w = parts[p]
-        b = bit(p, 0)
+        b = bit(i, p, 0)
         start = mine + i * R + (1 - b if late else b) * half
         blk = y_ref.at[pl.ds(pl.multiple_of(start, half), half), pl.ds(c0, w)]
         return pltpu.make_async_remote_copy(
@@ -120,7 +127,7 @@
         h[i, :, pl.ds(0, ff)] = hid[:R]
 
     def down(i):
-        slot = lax.rem(i, RING)
+        slot = lax.rem(i, RINGS[0])
         h_swap(i).wait_recv()
         for p in range(3):
             c0, w = parts[p]
@@ -132,49 +139,49 @@
             term = jnp.dot(
                 h[i], wd[:, c0 : c0 + w], preferred_element_type=jnp.float32
             )
-            b = bit(p, 0)
+            b = bit(i, p, 0)
             top, bot = term[:half], term[half:]
 
-            @pl.when(i >= RING)
+            @pl.when(i >= RINGS[0])
             def _():
-                hop(0, i - RING, p).wait_send()
+                hop(0, i - RINGS[0], p).wait_send()
 
             s1[slot, :, c0 : c0 + w] = jnp.where(b == 1, top, bot).astype(jnp.bfloat16)
             hop(0, i, p).start()
-            keep[slot, :, c0 : c0 + w] = jnp.where(b == 1, bot, top)
+            keep[i, :, c0 : c0 + w] = jnp.where(b == 1, bot, top)
 
     def reduce(stage, i):
-        slot = lax.rem(i, RING)
         for p in range(3):
             c0, w = parts[p]
             cols = pl.ds(c0, w)
             hop(stage, i, p).wait_recv()
-            b1, b2 = bit(p, 1), bit(p, 2)
+            b1, b2 = bit(i, p, 1), bit(i, p, 2)
+            kept = mine + i * R + bit(i, p, 0) * half
             if stage == 0:
                 o = pl.multiple_of((1 - b1) * quarter, quarter)
-                v = keep[slot, pl.ds(o, quarter), cols]
-                v = v + r1[i, pl.ds(o, quarter), cols].astype(jnp.float32)
-
-                @pl.when(i >= RING)
+                v = keep[i, pl.ds(o, quarter), cols]
+                v = v + y_ref[pl.ds(pl.multiple_of(kept + o, quarter), quarter), cols].astype(jnp.float32)
+
+                @pl.when(i >= RINGS[1])
                 def _():
-                    hop(1, i - RING, p).wait_send()
-
-                s2[slot, :, cols] = v.astype(jnp.bfloat16)
+                    hop(1, i - RINGS[1], p).wait_send()
+
+                s2[lax.rem(i, RINGS[1]), :, cols] = v.astype(jnp.bfloat16)
                 hop(1, i, p).start()
             else:
                 b = 1 - b2 if stage == 1 else b2
                 o1 = pl.multiple_of(b1 * quarter + b * eighth, eighth)
                 o2 = pl.multiple_of(b * eighth, eighth)
-                v = keep[slot, pl.ds(o1, eighth), cols]
-                v = v + r1[i, pl.ds(o1, eighth), cols].astype(jnp.float32)
+                v = keep[i, pl.ds(o1, eighth), cols]
+                v = v + y_ref[pl.ds(pl.multiple_of(kept + o1, eighth), eighth), cols].astype(jnp.float32)
                 v = v + r2[i, pl.ds(o2, eighth), cols].astype(jnp.float32)
                 if stage == 1:
 
-                    @pl.when(i >= RING)
+                    @pl.when(i >= RINGS[2])
                     def _():
-                        hop(2, i - RING, p).wait_send()
-
-                    s3[slot, :, cols] = v.astype(jnp.bfloat16)
+                        hop(2, i - RINGS[2], p).wait_send()
+
+                    s3[lax.rem(i, RINGS[2]), :, cols] = v.astype(jnp.bfloat16)
                     hop(2, i, p).start()
                 else:
                     v = v + r3[i, :, cols].astype(jnp.float32)
@@ -195,49 +202,56 @@
     wu_copy.start()
     wd_local.start()
     barrier = pltpu.get_barrier_semaphore()
-    for d in [partner] + across:
+    for d in [partner] + [me + s * (1 - 2 * lax.rem(lax.div(me, s), 2)) for s in (8, 4, 2)]:
         pl.semaphore_signal(barrier, inc=1, device_id=dev(d), device_id_type=MESH)
     pl.semaphore_wait(barrier, 4)
     for p in range(3):
         wd_swap(p).start()
     for c in x_copies(1):
         c.start()
-    wg_copy.wait()
-    wu_copy.wait()
-    gate_up(0)
-    wd_local.wait()
 
     def body(t, _):
-        for stage in (5, 4, 3):
-            i = t - 1 - stage
-
-            @pl.when(jnp.logical_and(i >= 0, i < n))
-            def _():
-                gather(stage, i)
-
-        for stage in (2, 1, 0):
-            i = t - 1 - stage
-
-            @pl.when(jnp.logical_and(i >= 0, i < n))
-            def _():
-                reduce(stage, i)
+        @pl.when(t == 0)
+        def _():
+            wg_copy.wait()
+            wu_copy.wait()
+
+        @pl.when(t == AHEAD)
+        def _():
+            wd_local.wait()
+
+        @pl.when(jnp.logical_and(t >= AHEAD, t < n + AHEAD))
+        def _():
+            down(t - AHEAD)
 
         @pl.when(t < n)
         def _():
-            down(t)
-
-        @pl.when(t + 1 < n)
-        def _():
+            gate_up(t)
+
             @pl.when(t + 2 < n)
             def _():
                 for c in x_copies(t + 2):
                     c.start()
 
-            gate_up(t + 1)
+        @pl.when(t > AHEAD)
+        def _():
+            reduce(0, t - AHEAD - 1)
 
         return 0
 
-    lax.fori_loop(0, n + 6, body, 0)
+    lax.fori_loop(0, n + AHEAD + 1, body, 0)
+
+    def each(f, stage):
+        def body(i, _):
+            f(stage, i)
+            return 0
+
+        lax.fori_loop(0, n, body, 0)
+
+    for stage in (1, 2):
+        each(reduce, stage)
+    for stage in (3, 4, 5):
+        each(gather, stage)
 
     for p in range(3):
         wd_swap(p).wait_send()
@@ -254,9 +268,9 @@
         return 0
 
     lax.fori_loop(0, n, drain, 0)
-    for i in range(n - RING, n):
-        for p in range(3):
-            for stage in range(3):
+    for stage in range(3):
+        for i in range(n - RINGS[stage], n):
+            for p in range(3):
                 hop(stage, i, p).wait_send()
 
 
@@ -283,11 +297,10 @@
                 pltpu.VMEM((2 * ff, d), bf16),
                 pltpu.VMEM((n, R, 2 * ff), bf16),
                 pltpu.VMEM((2, R, ff), bf16),
-                pltpu.VMEM((RING, R // 2, d), f32),
-                pltpu.VMEM((RING, R // 2, d), bf16),
-                pltpu.VMEM((RING, R // 4, d), bf16),
-                pltpu.VMEM((RING, R // 8, d), bf16),
-                pltpu.VMEM((n, R // 2, d), bf16),
+                pltpu.VMEM((n, R // 2, d), f32),
+                pltpu.VMEM((RINGS[0], R // 2, d), bf16),
+                pltpu.VMEM((RINGS[1], R // 4, d), bf16),
+                pltpu.VMEM((RINGS[2], R // 8, d), bf16),
                 pltpu.VMEM((n, R // 4, d), bf16),
                 pltpu.VMEM((n, R // 8, d), bf16),
                 dma((2, 2)),
@@ -305,7 +318,7 @@
             compiler_params=pltpu.CompilerParams(
                 collective_id=0,
                 has_side_effects=True,
-                vmem_limit_bytes=46 * 2**20,
+                vmem_limit_bytes=47 * 2**20,
             ),
             cost_estimate=pl.CostEstimate(
                 flops=6 * rows * d * ff, bytes_accessed=50 * 2**20, transcendentals=0

time: 139 us -> 135 us (0.971)
  Pallas kernels: 133 us -> 128 us
    pallas_call x1, Pallas kernels: 133 us -> 128 us  [step(): pl.pallas_call(functools.partial(kernel, (n, R, ff, parts)), name='mlp',...]
where the time goes in v2:
time: 135 us
  Pallas kernels  128 us (95%)
  local copies, waits for them, and re-layouts  6.16 us (5%)
    pallas_call x1, Pallas kernels, step(): pl.pallas_call(functools.partial(kernel, (n, R, ff, parts)), name='mlp',...  128 us
    unnamed x1, local copies, waits for them, and re-layouts  6.16 us

profile of v2, /device:TPU:0, one launch (start us, length us, event | category | flops | bytes accessed | tf_op | source)
XLA Modules:
  0.0 134.6 jit_solution(9256532886044770566)
XLA Ops:
  0.0 128.5 %mlp.1 = bf16[2048,4096]{1,0:T(8,128)(2,1)S(1)} custom-call(bf16[2048,4096]{1,0:T(8,128)(2,1)} %x_ref.1, bf16[4096,640]{1,0:T(8,128)(2,1)} %wg_ref.1, bf16[4096,640]{1,0:T(8,128)(2,1)} %wu_ref.1, bf16[640,4096]{1,0:T(8,128)(2,1)} %wd_ref.1), custom_call_target="tpu_custom_call" | custom-call | flops 32212254720 | bytes 52428800 | tf_op jit(solution)/shard_map/mlp/pallas_call | solution.py:288
  128.5 6.2 %copy.6 = bf16[2048,4096]{1,0:T(8,128)(2,1)} copy(bf16[2048,4096]{1,0:T(8,128)(2,1)S(1)} %mlp.1) | data formatting | bytes 33554432

commit v3 on v2

--- a/solution.py
+++ b/solution.py
@@ -9,7 +9,8 @@
 
 MESH = pl.DeviceIdType.MESH
 CHUNKS = 8
-AHEAD = 2
+LAGS = (3, 4, 5, 7, 9)
+KEEP = LAGS[2] - 1
 RINGS = (4, 4, 8)
 
 
@@ -52,8 +53,10 @@
             for j, start in enumerate((mine, other))
         ]
 
-    wg_copy = pltpu.make_async_copy(wg_ref, wgu.at[:, pl.ds(0, ff)], wsem.at[0])
-    wu_copy = pltpu.make_async_copy(wu_ref, wgu.at[:, pl.ds(ff, ff)], wsem.at[1])
+    w_copies = [
+        pltpu.make_async_copy(ref, wgu.at[:, pl.ds(j * ff, ff)], wsem.at[j])
+        for j, ref in enumerate((wg_ref, wu_ref))
+    ]
     wd_local = pltpu.make_async_copy(wd_ref, wd.at[pl.ds(0, ff), :], wdl.at[0])
 
     def wd_swap(p):
@@ -111,44 +114,65 @@
             device_id=dev(partner), device_id_type=MESH,
         )
 
+    def dot(a, b):
+        return jnp.dot(a, b, preferred_element_type=jnp.float32)
+
+    def hidden(gate, up, i):
+        slot = lax.rem(i, 2)
+        hid = (jax.nn.gelu(gate) * up).astype(jnp.bfloat16)
+        hs[slot] = hid[R:]
+        h_swap(i).start()
+        h[i, :, pl.ds(0, ff)] = hid[:R]
+
+    def gate_up_first():
+        for c in x_copies(0) + w_copies[:1]:
+            c.wait()
+        gate = dot(xb[0], wgu[:, :ff])
+        w_copies[1].wait()
+        hidden(gate, dot(xb[0], wgu[:, ff:]), 0)
+
     def gate_up(i):
         slot = lax.rem(i, 2)
         for c in x_copies(i):
             c.wait()
-        gu = jnp.dot(xb[slot], wgu[...], preferred_element_type=jnp.float32)
-        hid = (jax.nn.gelu(gu[:, :ff]) * gu[:, ff:]).astype(jnp.bfloat16)
 
         @pl.when(i >= 2)
         def _():
             h_swap(i - 2).wait_send()
 
-        hs[slot] = hid[R:]
-        h_swap(i).start()
-        h[i, :, pl.ds(0, ff)] = hid[:R]
+        gu = dot(xb[slot], wgu[...])
+        hidden(gu[:, :ff], gu[:, ff:], i)
+
+    def give(term, i, p):
+        c0, w = parts[p]
+        b = bit(i, p, 0)
+        top, bot = term[:half], term[half:]
+        s1[lax.rem(i, RINGS[0]), :, c0 : c0 + w] = jnp.where(b == 1, top, bot).astype(
+            jnp.bfloat16
+        )
+        hop(0, i, p).start()
+        keep[lax.rem(i, KEEP), :, c0 : c0 + w] = jnp.where(b == 1, bot, top)
+
+    def down_first():
+        h_swap(0).wait_recv()
+        wd_local.wait()
+        for p in range(3):
+            c0, w = parts[p]
+            wd_swap(p).wait_recv()
+            give(dot(h[0], wd[:, c0 : c0 + w]), 0, p)
 
     def down(i):
-        slot = lax.rem(i, RINGS[0])
         h_swap(i).wait_recv()
+
+        @pl.when(i >= RINGS[0])
+        def _():
+            for p in range(3):
+                hop(0, i - RINGS[0], p).wait_send()
+
+        term = dot(h[i], wd[...])
         for p in range(3):
             c0, w = parts[p]
-
-            @pl.when(i == 0)
-            def _():
-                wd_swap(p).wait_recv()
-
-            term = jnp.dot(
-                h[i], wd[:, c0 : c0 + w], preferred_element_type=jnp.float32
-            )
-            b = bit(i, p, 0)
-            top, bot = term[:half], term[half:]
-
-            @pl.when(i >= RINGS[0])
-            def _():
-                hop(0, i - RINGS[0], p).wait_send()
-
-            s1[slot, :, c0 : c0 + w] = jnp.where(b == 1, top, bot).astype(jnp.bfloat16)
-            hop(0, i, p).start()
-            keep[i, :, c0 : c0 + w] = jnp.where(b == 1, bot, top)
+            give(term[:, c0 : c0 + w], i, p)
 
     def reduce(stage, i):
         for p in range(3):
@@ -159,7 +183,7 @@
             kept = mine + i * R + bit(i, p, 0) * half
             if stage == 0:
                 o = pl.multiple_of((1 - b1) * quarter, quarter)
-                v = keep[i, pl.ds(o, quarter), cols]
+                v = keep[lax.rem(i, KEEP), pl.ds(o, quarter), cols]
                 v = v + y_ref[pl.ds(pl.multiple_of(kept + o, quarter), quarter), cols].astype(jnp.float32)
 
                 @pl.when(i >= RINGS[1])
@@ -172,7 +196,7 @@
                 b = 1 - b2 if stage == 1 else b2
                 o1 = pl.multiple_of(b1 * quarter + b * eighth, eighth)
                 o2 = pl.multiple_of(b * eighth, eighth)
-                v = keep[i, pl.ds(o1, eighth), cols]
+                v = keep[lax.rem(i, KEEP), pl.ds(o1, eighth), cols]
                 v = v + y_ref[pl.ds(pl.multiple_of(kept + o1, eighth), eighth), cols].astype(jnp.float32)
                 v = v + r2[i, pl.ds(o2, eighth), cols].astype(jnp.float32)
                 if stage == 1:
@@ -196,62 +220,65 @@
             if stage >= 4:
                 forward(i, p, stage - 4).start()
 
-    for c in x_copies(0):
+    for c in x_copies(0) + w_copies:
         c.start()
-    wg_copy.start()
-    wu_copy.start()
-    wd_local.start()
     barrier = pltpu.get_barrier_semaphore()
     for d in [partner] + [me + s * (1 - 2 * lax.rem(lax.div(me, s), 2)) for s in (8, 4, 2)]:
         pl.semaphore_signal(barrier, inc=1, device_id=dev(d), device_id_type=MESH)
     pl.semaphore_wait(barrier, 4)
     for p in range(3):
         wd_swap(p).start()
-    for c in x_copies(1):
+    for c in x_copies(1) + [wd_local]:
         c.start()
+    gate_up_first()
+    for c in x_copies(2):
+        c.start()
+
+    def step(stage, i):
+        (reduce if stage < 3 else gather)(stage, i)
 
     def body(t, _):
-        @pl.when(t == 0)
-        def _():
-            wg_copy.wait()
-            wu_copy.wait()
-
-        @pl.when(t == AHEAD)
-        def _():
-            wd_local.wait()
-
-        @pl.when(jnp.logical_and(t >= AHEAD, t < n + AHEAD))
-        def _():
-            down(t - AHEAD)
-
-        @pl.when(t < n)
-        def _():
-            gate_up(t)
-
-            @pl.when(t + 2 < n)
+        g = jnp.where(t < 2, t, t - 1)
+
+        @pl.when(jnp.logical_and(t != 2, g < n))
+        def _():
+            gate_up(g)
+
+            @pl.when(g + 2 < n)
             def _():
-                for c in x_copies(t + 2):
+                for c in x_copies(g + 2):
                     c.start()
 
-        @pl.when(t > AHEAD)
-        def _():
-            reduce(0, t - AHEAD - 1)
+        for stage, lag in enumerate(LAGS):
+
+            @pl.when(jnp.logical_and(t >= lag, t - lag < n))
+            def _():
+                step(stage, t - lag)
+
+        @pl.when(t == 1)
+        def _():
+            down_first()
+
+        @pl.when(jnp.logical_and(t > 1, t <= n))
+        def _():
+            down(t - 1)
 
         return 0
 
-    lax.fori_loop(0, n + AHEAD + 1, body, 0)
-
-    def each(f, stage):
+    last = n + LAGS[0] + 4
+    lax.fori_loop(1, last, body, 0)
+
+    def each(stage, start):
         def body(i, _):
-            f(stage, i)
+            step(stage, i)
             return 0
 
-        lax.fori_loop(0, n, body, 0)
-
-    for stage in (1, 2):
-        each(reduce, stage)
-    for stage in (3, 4, 5):
-        each(gather, stage)
+        lax.fori_loop(start, n, body, 0)
+
+    for stage, lag in enumerate(LAGS):
+        if last - lag < n:
+            each(stage, last - lag)
+    each(5, 0)
 
     for p in range(3):
         wd_swap(p).wait_send()
@@ -297,7 +324,7 @@
                 pltpu.VMEM((2 * ff, d), bf16),
                 pltpu.VMEM((n, R, 2 * ff), bf16),
                 pltpu.VMEM((2, R, ff), bf16),
-                pltpu.VMEM((n, R // 2, d), f32),
+                pltpu.VMEM((KEEP, R // 2, d), f32),
                 pltpu.VMEM((RINGS[0], R // 2, d), bf16),
                 pltpu.VMEM((RINGS[1], R // 4, d), bf16),
                 pltpu.VMEM((RINGS[2], R // 8, d), bf16),

time: 135 us -> 133 us (0.985)
  Pallas kernels: 128 us -> 126 us
    pallas_call x1, Pallas kernels: 128 us -> 126 us  [step(): pl.pallas_call(functools.partial(kernel, (n, R, ff, parts)), name='mlp',...]
where the time goes in v3:
time: 133 us
  Pallas kernels  126 us (95%)
  local copies, waits for them, and re-layouts  6.16 us (5%)
    pallas_call x1, Pallas kernels, step(): pl.pallas_call(functools.partial(kernel, (n, R, ff, parts)), name='mlp',...  126 us
    unnamed x1, local copies, waits for them, and re-layouts  6.16 us

profile of v3, /device:TPU:0, one launch (start us, length us, event | category | flops | bytes accessed | tf_op | source)
XLA Modules:
  0.0 132.7 jit_solution(2040743575339606623)
XLA Ops:
  0.0 126.5 %mlp.1 = bf16[2048,4096]{1,0:T(8,128)(2,1)S(1)} custom-call(bf16[2048,4096]{1,0:T(8,128)(2,1)} %x_ref.1, bf16[4096,640]{1,0:T(8,128)(2,1)} %wg_ref.1, bf16[4096,640]{1,0:T(8,128)(2,1)} %wu_ref.1, bf16[640,4096]{1,0:T(8,128)(2,1)} %wd_ref.1), custom_call_target="tpu_custom_call" | custom-call | flops 32212254720 | bytes 52428800 | tf_op jit(solution)/shard_map/mlp/pallas_call | solution.py:315
  126.5 6.2 %copy.6 = bf16[2048,4096]{1,0:T(8,128)(2,1)} copy(bf16[2048,4096]{1,0:T(8,128)(2,1)S(1)} %mlp.1) | data formatting | bytes 33554432

commit v4 on v3

--- a/solution.py
+++ b/solution.py
@@ -17,7 +17,7 @@
 def kernel(
     cfg, x_ref, wg_ref, wu_ref, wd_ref, y_ref,
     xb, wgu, wd, h, hs, keep, s1, s2, s3, r2, r3,
-    xsem, wsem, wdl, wds, wdr, hss, hsr, ss, rs, fs, fr,
+    xsem, wsem, wdl, wds, wdr, hss, hsr, ss, rs, gs, fs, fr,
 ):
     n, R, ff, parts = cfg
     half, quarter, eighth = R // 2, R // 4, R // 8
@@ -71,7 +71,7 @@
         return pltpu.make_async_remote_copy(
             hs.at[lax.rem(i, 2)],
             h.at[i, :, pl.ds(ff, ff)],
-            hss.at[i], hsr.at[i], device_id=dev(partner), device_id_type=MESH,
+            hss.at[lax.rem(i, 2)], hsr.at[i], device_id=dev(partner), device_id_type=MESH,
         )
 
     def y_rows(i, p, depth):
@@ -87,6 +87,7 @@
         cols = pl.ds(c0, w)
         if stage < 3:
             slot = lax.rem(i, RINGS[stage])
+            sent = ss.at[sum(RINGS[:stage]) + slot, p]
         if stage == 0:
             k = 0
             src = s1.at[slot, :, cols]
@@ -99,8 +100,9 @@
         else:
             k = 5 - stage
             src = dst = y_ref.at[y_rows(i, p, k + 1), cols]
-        return pltpu.make_async_remote_copy(
-            src, dst, ss.at[stage, i, p], rs.at[stage, i, p],
+            sent = gs
+        return pltpu.make_async_remote_copy(
+            src, dst, sent, rs.at[stage, i, p],
             device_id=to(i, p, k), device_id_type=MESH,
         )
 
@@ -110,7 +112,7 @@
         start = mine + i * R + (1 - b if late else b) * half
         blk = y_ref.at[pl.ds(pl.multiple_of(start, half), half), pl.ds(c0, w)]
         return pltpu.make_async_remote_copy(
-            blk, blk, fs.at[late, i, p], fr.at[late, i, p],
+            blk, blk, fs, fr,
             device_id=dev(partner), device_id_type=MESH,
         )
 
@@ -127,9 +129,12 @@
     def gate_up_first():
         for c in x_copies(0) + w_copies[:1]:
             c.wait()
+        for c in [wd_local] + x_copies(1):
+            c.start()
         gate = dot(xb[0], wgu[:, :ff])
         w_copies[1].wait()
         hidden(gate, dot(xb[0], wgu[:, ff:]), 0)
+        wd_swap(2).start()
 
     def gate_up(i):
         slot = lax.rem(i, 2)
@@ -226,10 +231,8 @@
     for d in [partner] + [me + s * (1 - 2 * lax.rem(lax.div(me, s), 2)) for s in (8, 4, 2)]:
         pl.semaphore_signal(barrier, inc=1, device_id=dev(d), device_id_type=MESH)
     pl.semaphore_wait(barrier, 4)
-    for p in range(3):
+    for p in range(2):
         wd_swap(p).start()
-    for c in x_copies(1) + [wd_local]:
-        c.start()
     gate_up_first()
     for c in x_copies(2):
         c.start()
@@ -285,20 +288,45 @@
     for i in range(n - 2, n):
         h_swap(i).wait_send()
 
-    def drain(i, _):
-        for p in range(3):
-            for stage in range(3, 6):
-                hop(stage, i, p).wait_send()
-            for late in range(2):
-                forward(i, p, late).wait_send()
-                forward(i, p, late).wait_recv()
-        return 0
-
-    lax.fori_loop(0, n, drain, 0)
+    def all_of(count, sent, arrived):
+        blk = y_ref.at[pl.ds(0, count), :]
+        return pltpu.make_async_remote_copy(
+            blk, blk, sent, arrived, device_id=dev(partner), device_id_type=MESH
+        )
+
+    all_of(rows - rows // 8, gs, fr).wait_send()
+    all_of(rows, fs, fr).wait()
     for stage in range(3):
         for i in range(n - RINGS[stage], n):
             for p in range(3):
                 hop(stage, i, p).wait_send()
+
+
+def store(y):
+    pieces = 8
+
+    def body(y_ref, o_ref, sem):
+        rows = y.shape[0] // pieces
+        copies = [
+            pltpu.make_async_copy(
+                y_ref.at[pl.ds(i * rows, rows)], o_ref.at[pl.ds(i * rows, rows)], sem.at[i]
+            )
+            for i in range(pieces)
+        ]
+        for c in copies:
+            c.start()
+        for c in copies:
+            c.wait()
+
+    return pl.pallas_call(
+        body,
+        name="store",
+        out_shape=jax.ShapeDtypeStruct(y.shape, y.dtype),
+        in_specs=[pl.BlockSpec(memory_space=pltpu.VMEM)],
+        out_specs=pl.BlockSpec(memory_space=pltpu.HBM),
+        scratch_shapes=[pltpu.SemaphoreType.DMA((pieces,))],
+        compiler_params=pltpu.CompilerParams(vmem_limit_bytes=2**20),
+    )(y)
 
 
 def solution(mesh):
@@ -312,7 +340,7 @@
         parts = tuple((sum(widths[:p]), widths[p]) for p in range(3))
         bf16, f32 = jnp.bfloat16, jnp.float32
         dma = pltpu.SemaphoreType.DMA
-        return pl.pallas_call(
+        y = pl.pallas_call(
             functools.partial(kernel, (n, R, ff, parts)),
             name="mlp",
             out_shape=pltpu.VMEM((rows, d), bf16),
@@ -335,12 +363,13 @@
                 dma((1,)),
                 dma((3,)),
                 dma((3,)),
+                dma((2,)),
                 dma((n,)),
-                dma((n,)),
+                dma((sum(RINGS), 3)),
                 dma((6, n, 3)),
-                dma((6, n, 3)),
-                dma((2, n, 3)),
-                dma((2, n, 3)),
+                dma,
+                dma,
+                dma,
             ],
             compiler_params=pltpu.CompilerParams(
                 collective_id=0,
@@ -351,6 +380,7 @@
                 flops=6 * rows * d * ff, bytes_accessed=50 * 2**20, transcendentals=0
             ),
         )(x, w_gate, w_up, w_down)
+        return store(y)
 
     return jax.shard_map(
         step,

time: 133 us -> 130 us (0.977)
  local copies, waits for them, and re-layouts: 6.16 us -> 0 us
  Pallas kernels: 126 us -> 130 us
    unnamed x1 -> x0, local copies, waits for them, and re-layouts: 6.16 us -> none
    pallas_call x0 -> x1, Pallas kernels: none -> 5.92 us  [store(): pl.pallas_call(body, name='store', out_shape=jax.ShapeDtypeStruct(y.shape...]
    pallas_call x1, Pallas kernels: 126 us -> 124 us  [step(): pl.pallas_call(functools.partial(kernel, (n, R, ff, parts)), name='mlp',...]
where the time goes in v4:
time: 130 us
  Pallas kernels  130 us (100%)
    pallas_call x1, Pallas kernels, step(): pl.pallas_call(functools.partial(kernel, (n, R, ff, parts)), name='mlp',...  124 us
    pallas_call x1, Pallas kernels, store(): pl.pallas_call(body, name='store', out_shape=jax.ShapeDtypeStruct(y.shape...  5.92 us

profile of v4, /device:TPU:0, one launch (start us, length us, event | category | flops | bytes accessed | tf_op | source)
XLA Modules:
  0.0 129.9 jit_solution(4222776016163454738)
XLA Ops:
  0.0 124.0 %mlp.1.y_ref = bf16[2048,4096]{1,0:T(8,128)(2,1)S(1)} custom-call(bf16[2048,4096]{1,0:T(8,128)(2,1)} %x_ref.1, bf16[4096,640]{1,0:T(8,128)(2,1)} %wg_ref.1, bf16[4096,640]{1,0:T(8,128)(2,1)} %wu_ref.1, bf16[640,4096]{1,0:T(8,128)(2,1)} %wd_ref.1), custom_call_target="tpu_custom_call" | custom-call | flops 32212254720 | bytes 52428800 | tf_op jit(solution)/shard_map/mlp/pallas_call | solution.py:343
  124.0 5.9 %store.1 = bf16[2048,4096]{1,0:T(8,128)(2,1)} custom-call(bf16[2048,4096]{1,0:T(8,128)(2,1)S(1)} %mlp.1.y_ref), custom_call_target="tpu_custom_call" | custom-call | tf_op jit(solution)/shard_map/store/pallas_call | solution.py:321
